TPU v7x, 32 devices: a whole 2x2x4 slice. The times are simulated.
32 devices in a mesh: rep: 1, dp: 32 (over x, y, z, core).
Axes of the slice: x: 2, y: 2, z: 4, core: 2. Of those that a mesh axis runs over, the one named last changes fastest.
Arguments:
- g_w_gate: bfloat16 [32, 2, 1280, 3072], P(('rep', 'dp'))
- g_w_up: bfloat16 [32, 2, 1280, 3072], P(('rep', 'dp'))
- g_w_down: bfloat16 [32, 2, 3072, 1280], P(('rep', 'dp'))
- w_gate: bfloat16 [2, 1280, 3072], replicated
- w_up: bfloat16 [2, 1280, 3072], replicated
- w_down: bfloat16 [2, 3072, 1280], replicated
- m_w_gate: float32 [2, 1280, 3072], P(None, 'dp')
- m_w_up: float32 [2, 1280, 3072], P(None, 'dp')
- m_w_down: float32 [2, 3072, 1280], P(None, 'dp')
- v_w_gate: float32 [2, 1280, 3072], P(None, 'dp')
- v_w_up: float32 [2, 1280, 3072], P(None, 'dp')
- v_w_down: float32 [2, 3072, 1280], P(None, 'dp')
Outputs:
- output 1: bfloat16 [2, 1280, 3072], P('rep')
- output 2: bfloat16 [2, 1280, 3072], P('rep')
- output 3: bfloat16 [2, 3072, 1280], P('rep')
- output 4: float32 [2, 1280, 3072], P('rep', 'dp')
- output 5: float32 [2, 1280, 3072], P('rep', 'dp')
- output 6: float32 [2, 3072, 1280], P('rep', 'dp')
- output 7: float32 [2, 1280, 3072], P('rep', 'dp')
- output 8: float32 [2, 1280, 3072], P('rep', 'dp')
- output 9: float32 [2, 3072, 1280], P('rep', 'dp')
All inputs are finite; a program needn't handle non-finite values.
Results may differ from a plain program's by a relative error of at most 0.022.
Values are sent between devices in bfloat16 or wider.
A program may use at most 2 GiB of HBM per device.

v0:
```python
import jax
import jax.numpy as jnp
from jax import lax
from jax.sharding import PartitionSpec as P


def adamw(w, m, v, g):
    m = 0.9 * m + 0.1 * g
    v = 0.95 * v + 0.05 * g * g
    step = m * lax.rsqrt(v + 1e-8) + 0.1 * w
    return (w - 0.02 * step).astype(jnp.bfloat16), m, v


def solution(mesh):
    def step(*arrays):
        terms, weights, m, v = (arrays[i : i + 3] for i in (0, 3, 6, 9))
        gradients = [lax.psum_scatter(t[0], "dp", scatter_dimension=1, tiled=True).astype(jnp.float32) for t in terms]
        me = lax.axis_index("dp")
        own = [lax.dynamic_slice_in_dim(w, me * one.shape[1], one.shape[1], 1).astype(jnp.float32) for w, one in zip(weights, m, strict=True)]
        new = [adamw(w, m, v, g) for w, m, v, g in zip(own, m, v, gradients, strict=True)]
        whole = [lax.all_gather(one[0], "dp", axis=1, tiled=True) for one in new]
        return (*whole, *(one[1] for one in new), *(one[2] for one in new))

    all_of, cut = P(None, None, None), P(None, "dp", None)
    return jax.shard_map(
        step,
        mesh=mesh,
        in_specs=(P(("rep", "dp"), None, None, None),) * 3 + (all_of,) * 3 + (cut,) * 6,
        out_specs=(P("rep", None, None),) * 3 + (P("rep", "dp", None),) * 6,
        check_vma=False,
    )
```

profile of v0, /device:TPU:0, one launch (start us, length us, event | category | flops | bytes accessed | tf_op | source)
XLA Modules:
  0.0 915.9 jit_solution(1003807580396736472)
XLA Ops:
  7.2 0.0 reduce-scatter.8.cloned.1.call-start
  7.2 0.7 reduce-scatter.8.cloned.1.call-update
  7.9 0.0 reduce-scatter.10.cloned.1.call-start
  8.0 28.4 %copy.21 = bf16[2,1280,3072]{2,0,1:T(2,128)(2,1)S(1)} copy(bf16[2,1280,3072]{2,1,0:T(8,128)(2,1)} %bitcast.15) | data formatting | bytes 31457280
  36.4 7.6 copy.25
  44.0 0.0 reduce-scatter.10.cloned.1.call-update
  44.0 0.0 reduce-scatter.12.cloned.1.call-start
  44.1 28.4 %copy.23 = bf16[2,1280,3072]{2,0,1:T(2,128)(2,1)S(1)} copy(bf16[2,1280,3072]{2,1,0:T(8,128)(2,1)} %bitcast.16) | data formatting | bytes 31457280
  72.5 7.6 copy.26
  80.1 0.0 copy-start.1
  80.1 0.0 copy-start.2
  80.1 0.0 copy-start.3
  80.1 0.0 reduce-scatter.12.cloned.1.call-update
  80.2 0.0 all-gather.8.cloned.1.call-start
  80.2 106.8 %reduce-scatter.8.cloned.1.call-done = bf16[2,96,1280]{2,1,0:T(8,128)(2,1)} async-done(((bf16[2,3072,1280]{2,1,0:T(8,128)(2,1)}), bf16[2,96,1280]{2,1,0:T(8,128)(2,1)}) %reduce-scatter.8.cloned.1.call-update) | async-done | bytes 491536 | tf_op jit(solution)/shard_map/reduce_scatter | solution.py:17
  187.0 0.0 copy-done.1
  187.0 0.0 copy-done.2
  187.0 2.8 fusion.10
  189.8 0.0 all-gather.8.cloned.1.call-update
  189.9 0.0 all-gather.4.cloned.1.call-start
  189.9 174.0 %reduce-scatter.10.cloned.1.call-done = bf16[40,6144]{1,0:T(8,128)(2,1)} async-done(((bf16[1280,6144]{1,0:T(8,128)(2,1)}), bf16[40,6144]{1,0:T(8,128)(2,1)}) %reduce-scatter.10.cloned.1.call-update) | async-done | bytes 491536
  363.9 1.4 reshape.19
  365.3 0.0 copy-done.3
  365.3 3.1 fusion.2
  368.4 0.0 all-gather.4.cloned.1.call-update
  368.4 0.0 all-gather.6.cloned.1.call-start
  368.5 172.4 %reduce-scatter.12.cloned.1.call-done = bf16[40,6144]{1,0:T(8,128)(2,1)} async-done(((bf16[1280,6144]{1,0:T(8,128)(2,1)}), bf16[40,6144]{1,0:T(8,128)(2,1)}) %reduce-scatter.12.cloned.1.call-update) | async-done | bytes 491536
  540.9 1.4 reshape.21
  542.3 3.4 fusion.6
  545.7 0.0 all-gather.6.cloned.1.call-update
  545.7 108.4 %all-gather.8.cloned.1.call-done = bf16[2,3072,1280]{2,1,0:T(8,128)(2,1)} async-done(((bf16[2,96,1280]{2,1,0:T(8,128)(2,1)}), bf16[2,3072,1280]{2,1,0:T(8,128)(2,1)}) %all-gather.8.cloned.1.call-update) | async-done | bytes 15728656 | tf_op jit(solution)/shard_map/all_gather | solution.py:21
  654.1 111.4 %all-gather.4.cloned.1.call-done = bf16[2,1280,3072]{2,1,0:T(8,128)(2,1)} async-done(((bf16[2,40,3072]{2,1,0:T(8,128)(2,1)}), bf16[2,1280,3072]{2,1,0:T(8,128)(2,1)}) %all-gather.4.cloned.1.call-update) | async-done | bytes 15728656 | tf_op jit(solution)/shard_map/all_gather | solution.py:21
  765.5 111.4 %all-gather.6.cloned.1.call-done = bf16[2,1280,3072]{2,1,0:T(8,128)(2,1)} async-done(((bf16[2,40,3072]{2,1,0:T(8,128)(2,1)}), bf16[2,1280,3072]{2,1,0:T(8,128)(2,1)}) %all-gather.6.cloned.1.call-update) | async-done | bytes 15728656 | tf_op jit(solution)/shard_map/all_gather | solution.py:21
  877.0 0.0 copy-start
  877.0 0.0 slice-start
  877.0 0.0 slice-start.1
  877.0 15.9 %copy.38 = bf16[2,1280,3072]{2,1,0:T(8,128)(2,1)} copy(bf16[2,1280,3072]{2,1,0:T(8,128)(2,1)} %all-gather.4.cloned.1.call-done) | data formatting | bytes 31457280
  892.8 0.0 copy-done
  892.8 0.0 slice-start.2
  892.8 0.0 slice-start.3
  892.8 8.0 copy.39
  900.8 0.0 slice-done
  900.8 0.0 slice-done.1
  900.8 1.5 slice-done.2
  902.3 0.9 slice-done.3
  903.2 5.8 copy.40
  (1 shorter events, 0.0 us)
Async XLA Ops:
  7.2 179.8 %reduce-scatter.8.cloned.1.call-start = ((), (), s32[]{:S(2)}) async-start(), calls=%async_computation.5 | async-start | bytes 16220160 | tf_op jit(solution)/shard_map/reduce_scatter | solution.py:17
  7.9 356.0 %reduce-scatter.10.cloned.1.call-start = ((), (), s32[]{:S(2)}) async-start(), calls=%async_computation.7 | async-start | bytes 16220160
  44.0 496.8 %reduce-scatter.12.cloned.1.call-start = ((), (), s32[]{:S(2)}) async-start(), calls=%async_computation.8 | async-start | bytes 16220160
  80.1 106.9 %copy-start.1 = (f32[2,96,1280]{2,1,0:T(8,128)S(1)}, f32[2,96,1280]{2,1,0:T(8,128)}, u32[]{:S(2)}) copy-start(f32[2,96,1280]{2,1,0:T(8,128)} %param.23) | copy-start | bytes 2949124
  80.1 106.9 %copy-start.2 = (f32[2,96,1280]{2,1,0:T(8,128)S(1)}, f32[2,96,1280]{2,1,0:T(8,128)}, u32[]{:S(2)}) copy-start(f32[2,96,1280]{2,1,0:T(8,128)} %param.20) | copy-start | bytes 2949124
  80.1 285.2 %copy-start.3 = (f32[2,40,3072]{2,1,0:T(8,128)S(1)}, f32[2,40,3072]{2,1,0:T(8,128)}, u32[]{:S(2)}) copy-start(f32[2,40,3072]{2,1,0:T(8,128)} %param.21) | copy-start | bytes 2949124
  80.2 573.9 %all-gather.8.cloned.1.call-start = ((), (), s32[]{:S(2)}) async-start(), calls=%async_computation.6 | async-start | bytes 16220160 | tf_op jit(solution)/shard_map/all_gather | solution.py:21
  189.9 575.6 %all-gather.4.cloned.1.call-start = ((), (), s32[]{:S(2)}) async-start(), calls=%async_computation.3 | async-start | bytes 16220160 | tf_op jit(solution)/shard_map/all_gather | solution.py:21
  368.4 508.5 %all-gather.6.cloned.1.call-start = ((), (), s32[]{:S(2)}) async-start(), calls=%async_computation.4 | async-start | bytes 16220160 | tf_op jit(solution)/shard_map/all_gather | solution.py:21
  877.0 15.9 %copy-start = (bf16[2,1280,3072]{2,1,0:T(8,128)(2,1)S(1)}, bf16[2,1280,3072]{2,1,0:T(8,128)(2,1)}, u32[]{:S(2)}) copy-start(bf16[2,1280,3072]{2,1,0:T(8,128)(2,1)} %all-gather.6.cloned.1.call-done) | copy-start | bytes 47185924
  877.0 23.8 %slice-start = ((s8[15728640]{0:T(1024)(128)(4,1)}), s8[4194304]{0:T(1024)(128)(4,1)S(1)}, s32[]{:S(2)}) async-start(s8[15728640]{0:T(1024)(128)(4,1)} %bitcast.18), calls=%async_computation.9 | async-start | bytes 8388608
  877.0 23.8 %slice-start.1 = ((s8[15728640]{0:T(1024)(128)(4,1)}), s8[4194304]{0:T(1024)(128)(4,1)S(1)}, s32[]{:S(2)}) async-start(s8[15728640]{0:T(1024)(128)(4,1)} %bitcast.18), calls=%async_computation.10 | async-start | bytes 8388608
  892.8 9.5 %slice-start.2 = ((s8[15728640]{0:T(1024)(128)(4,1)}), s8[4194304]{0:T(1024)(128)(4,1)S(1)}, s32[]{:S(2)}) async-start(s8[15728640]{0:T(1024)(128)(4,1)} %bitcast.18), calls=%async_computation.11 | async-start | bytes 8388608
  892.8 10.4 %slice-start.3 = ((s8[15728640]{0:T(1024)(128)(4,1)}), s8[3145728]{0:T(1024)(128)(4,1)S(1)}, s32[]{:S(2)}) async-start(s8[15728640]{0:T(1024)(128)(4,1)} %bitcast.18), calls=%async_computation.12 | async-start | bytes 6291456
Sparse Core Ops, SparseCore 0:
  14.0 172.9 reduce-scatter.7
  193.6 170.2 reduce-scatter.9
  370.5 170.3 reduce-scatter.11
  544.4 109.6 all-gather.7
  657.6 107.9 all-gather.3
  769.0 107.9 all-gather.5
where the time goes:
time: 916 us
  waiting for transfers between devices  785 us (86%)
  local copies, waits for them, and re-layouts  107 us (12%)
  between operations  14.2 us (2%)
  other arithmetic  9.33 us (1%)
    unnamed x8, waiting for transfers between devices  347 us
    all_gather x3, waiting for transfers between devices, step(): whole = [lax.all_gather(one[0], 'dp', axis=1, tiled=True) for one in new]  331 us
    unnamed x25, local copies, waits for them, and re-layouts  107 us
    reduce_scatter x1, waiting for transfers between devices, step(): lax.psum_scatter(t[0], 'dp', scatter_dimension=1, tiled=True)  107 us
  transfers between devices with their start and end apart: 6, of which 6 were waited for; matrix products, arithmetic and copies ran while one was open for 9% of the time, Pallas kernels for 0%

commit v1 on v0

v1 whole, which is shorter than its diff:
```python
import functools

import jax
import jax.numpy as jnp
from jax import lax
from jax.experimental import pallas as pl
from jax.experimental.pallas import tpu as pltpu
from jax.sharding import PartitionSpec as P

TILES = 120
CUT = 60
GROUP = 12
SLOTS = 6
F32, BF16 = jnp.float32, jnp.bfloat16


def tiled(a, lead, rows, columns):
    a = a.reshape(2, *lead, rows // 8, 8, columns // 128, 128)
    return jnp.swapaxes(a, a.ndim - 3, a.ndim - 2).reshape(2, *lead, TILES, 8, 128)


def untiled(a, rows, columns):
    n = a.size // (2 * rows * columns)
    a = a.reshape(2, n, rows // 8, columns // 128, 8, 128)
    return jnp.swapaxes(a, 3, 4).reshape(2, n * rows, columns)


def chunks():
    return [(k, l, o) for k in range(3) for l in range(2) for o in range(0, TILES, CUT)]


def kernel(*refs):
    g, w, m, v = (refs[i : i + 3] for i in (0, 3, 6, 9))
    out, new_m, new_v, r0 = (refs[i : i + 3] for i in (12, 15, 18, 21))
    po, t0, kg, kr, r1, r2, r3, wb, mb, vb = refs[24:34]
    (p0s, p0r, lg, lt, lk, lm, p1s, p1r, zs, zr, p3s, p3r, a3s, a3r, gs, gr, a1s, a1r, a0s, a0r, loc, st) = refs[34:]
    todo = chunks()
    n = len(todo)

    me = lax.axis_index("dp")
    core, z, y, x = me % 2, me // 2 % 4, me // 8 % 2, me // 16
    a, b = x * (1 - core) + y * core, y * (1 - core) + x * core
    sa, sb = 2 - core, 1 + core
    far = z // 2
    turn = 1 - 2 * far
    here = z * turn + 3 * far
    outer, inner = here == 0, here == 1
    partner = me + 1 - 2 * core
    beside_a = ((1 - a) * sa + b * sb) * 8 + z * 2 + core
    beside_b = (a * sa + (1 - b) * sb) * 8 + z * 2 + core
    inward, outward = me + 2 * turn, me - 2 * turn

    def xy(one_a, one_b):
        return one_a * sa + one_b * sb

    def along(t):
        return t * turn + 3 * far

    def remote(src, dst, send, recv, device):
        return pltpu.make_async_remote_copy(
            src_ref=src, dst_ref=dst, send_sem=send, recv_sem=recv, device_id={"dp": device}, device_id_type=pl.DeviceIdType.MESH
        )

    def await_(ref, sem):
        pltpu.make_async_copy(ref, ref, sem).wait()

    def part(c):
        return pl.ds(todo[c][2], CUT)

    def add(dst, *terms):
        @pl.loop(0, CUT // GROUP)
        def _(i):
            at = pl.ds(i * GROUP, GROUP)
            total = terms[0][at].astype(F32)
            for term in terms[1:]:
                total = total + term[at].astype(F32)
            dst[at] = total.astype(BF16)

    def p0(c):
        k, l, _ = todo[c]
        return remote(g[k].at[l, :, :, 1 - core, part(c)], r0[k].at[l, :, :, part(c)], p0s.at[c], p0r.at[c], partner)

    def load_out(c):
        k, l, _ = todo[c]
        return [pltpu.make_async_copy(g[k].at[l, xy(1 - a, j), :, core, part(c)], po.at[c, j], lg.at[c, j]) for j in range(2)]

    def load_out_r0(c):
        k, l, _ = todo[c]
        return [pltpu.make_async_copy(r0[k].at[l, xy(1 - a, j), :, part(c)], t0.at[c % 3, j], lt.at[c % 3, j]) for j in range(2)]

    def load_kept(c):
        k, l, _ = todo[c]
        s = c % SLOTS
        return [pltpu.make_async_copy(g[k].at[l, xy(a, j), :, core, part(c)], kg.at[s, j], lk.at[s, j]) for j in range(2)] + [
            pltpu.make_async_copy(r0[k].at[l, xy(a, j), :, part(c)], kr.at[s, j], lk.at[s, 2 + j]) for j in range(2)
        ]

    def load_state(c):
        k, l, _ = todo[c]
        return [
            pltpu.make_async_copy(w[k].at[l, x * 2 + y, z, core, part(c)], wb.at[c], lm.at[c, 0]),
            pltpu.make_async_copy(m[k].at[l, part(c)], mb.at[c], lm.at[c, 1]),
            pltpu.make_async_copy(v[k].at[l, part(c)], vb.at[c], lm.at[c, 2]),
        ]

    def store_state(c):
        k, l, _ = todo[c]
        return [
            pltpu.make_async_copy(mb.at[c], new_m[k].at[l, part(c)], st.at[c, 0]),
            pltpu.make_async_copy(vb.at[c], new_v[k].at[l, part(c)], st.at[c, 1]),
        ]

    def p1(c):
        return remote(po.at[c], r1.at[c], p1s.at[c], p1r.at[c], beside_a)

    def zsend(c, i, t, slot, device):
        return remote(kg.at[c % SLOTS, :, along(t)], r2.at[c, slot], zs.at[c, i], zr.at[c, slot], device)

    def p3(c):
        return remote(kg.at[c % SLOTS, 1 - b, z], r3.at[c], p3s.at[c], p3r.at[c], beside_b)

    def a3(c):
        return remote(r1.at[c, b, z], r1.at[c, b, z], a3s.at[c], a3r.at[c], beside_b)

    def gsend(c, i, t, slot, device):
        where = r1.at[c, :, along(t)]
        return remote(where, where, gs.at[c, i], gr.at[c, slot], device)

    def spread(c, t):
        k, l, _ = todo[c]
        for j in range(2):
            src, dst = r1.at[c, j, t], out[k].at[l, xy(a, j), t, core, part(c)]
            remote(src, dst, a1s.at[c], a1r.at[c], beside_a).start()
            remote(src, dst, a0s.at[c], a0r.at[c], partner).start()
            pltpu.make_async_copy(src, dst, loc.at[c]).start()

    def relay(c):
        k, l, _ = todo[c]
        for j in range(2):
            where = out[k].at[l, xy(1 - a, j), :, core, part(c)]
            remote(where, where, a0s.at[c], a0r.at[c], partner).start()

    def kept_terms(c, j, t, *slots):
        s = c % SLOTS
        return (kg.at[s, j, t], kr.at[s, j, t], r1.at[c, j, t], *(r2.at[c, i, j] for i in slots))

    def sum_piece(c, t, *slots):
        for j in range(2):
            add(kg.at[c % SLOTS, j, along(t)], *kept_terms(c, j, along(t), *slots))

    freed, ready = set(range(SLOTS)), set()

    def maybe_load(c):
        if c in freed and c in ready:
            for one in load_kept(c):
                one.start()

    def step_l(c):
        await_(r0[todo[c][0]].at[todo[c][1], :, :, part(c)], p0r.at[c])
        for one in load_out_r0(c):
            one.start()
        ready.add(c)
        maybe_load(c)

    def step_e(c):
        for one in load_out(c) + load_out_r0(c):
            one.wait()

        @pl.loop(0, 8)
        def _(i):
            add(po.at[c, i // 4, i % 4], po.at[c, i // 4, i % 4], t0.at[c % 3, i // 4, i % 4])

        p1(c).start()

    def step_z0(c):
        for one in load_kept(c):
            one.wait()
        await_(r1.at[c], p1r.at[c])

        @pl.when(outer)
        def _():
            for i, t in enumerate((3, 2, 1)):
                sum_piece(c, t)
                zsend(c, i, t, i, inward).start()

    def step_z1(c):
        @pl.when(inner)
        def _():
            await_(r2.at[c, 0], zr.at[c, 0])
            sum_piece(c, 3, 0)
            zsend(c, 0, 3, 3, inward).start()

    def step_z2(c):
        @pl.when(inner)
        def _():
            await_(r2.at[c, 1], zr.at[c, 1])
            sum_piece(c, 2, 1)
            zsend(c, 1, 2, 4, inward).start()

    def step_z3(c):
        @pl.when(inner)
        def _():
            await_(r2.at[c, 3], zr.at[c, 3])
            sum_piece(c, 0, 3)
            zsend(c, 2, 0, 3, outward).start()

    def step_f(c):
        @pl.when(outer)
        def _():
            await_(r2.at[c, 3], zr.at[c, 3])
            add(kg.at[c % SLOTS, 1 - b, z], *kept_terms(c, 1 - b, z, 3))

        @pl.when(inner)
        def _():
            await_(r2.at[c, 2], zr.at[c, 2])
            await_(r2.at[c, 4], zr.at[c, 4])
            add(kg.at[c % SLOTS, 1 - b, z], *kept_terms(c, 1 - b, z, 2, 4))

        p3(c).start()

    def step_g(c):
        await_(r3.at[c], p3r.at[c])
        gradient = kg.at[c % SLOTS, b, z]

        @pl.when(outer)
        def _():
            add(gradient, *kept_terms(c, b, z, 3), r3.at[c])

        @pl.when(inner)
        def _():
            add(gradient, *kept_terms(c, b, z, 2, 4), r3.at[c])

        for one in load_state(c):
            one.wait()

        @pl.loop(0, CUT // GROUP)
        def _(i):
            at = pl.ds(i * GROUP, GROUP)
            grad = gradient[at].astype(F32)
            one_m = 0.9 * mb[c, at] + 0.1 * grad
            one_v = 0.95 * vb[c, at] + 0.05 * grad * grad
            one_w = wb[c, at].astype(F32)
            mb[c, at] = one_m
            vb[c, at] = one_v
            r1[c, b, z, at] = (one_w - 0.02 * (one_m * lax.rsqrt(one_v + 1e-8) + 0.1 * one_w)).astype(BF16)

        a3(c).start()
        for one in store_state(c):
            one.start()

    def step_h(c):
        await_(r1.at[c, 1 - b, z], a3r.at[c])

        @pl.when(outer)
        def _():
            gsend(c, 0, 0, 0, inward).start()

        @pl.when(inner)
        def _():
            gsend(c, 0, 1, 0, outward).start()
            gsend(c, 1, 1, 1, inward).start()

        spread(c, z)

    def step_r(c):
        for i in range(3):
            await_(kg.at[c % SLOTS, :, 0], zs.at[c, i])
        await_(r3.at[c], p3s.at[c])
        freed.add(c + SLOTS)
        maybe_load(c + SLOTS)

    def step_i(c, i):
        @pl.when(outer)
        def _():
            await_(r1.at[c, :, along(i + 1)], gr.at[c, i])
            spread(c, along(i + 1))

        @pl.when(inner)
        def _():
            t = (0, 2, 3)[i]
            await_(r1.at[c, :, along(t)], gr.at[c, i])
            if i == 0:
                gsend(c, 2, 0, 2, inward).start()
            else:
                gsend(c, 2 + i, t, i, outward).start()
            spread(c, along(t))

    def step_k(c):
        await_(r1.at[c], a1r.at[c])
        relay(c)

    unit = CUT / 60
    events = []
    for c in range(n):
        first = (18 + 16 * c) * unit
        events.append(((5 + 4 * (c - 1)) * unit, step_l, (c,)))
        events.append(((6 + 4 * c) * unit, step_e, (c,)))
        events.append((first, step_z0, (c,)))
        events.append((first + 8 * unit, step_z1, (c,)))
        events.append((first + 14 * unit, step_z2, (c,)))
        events.append((first + 14.1 * unit, step_z3, (c,)))
        events.append((first + 21 * unit, step_f, (c,)))
        events.append((first + 25 * unit, step_g, (c,)))
        events.append((first + 29 * unit, step_h, (c,)))
        events.append((first + 31 * unit, step_r, (c,)))
        for i in range(3):
            events.append((first + (37 + 7 * i) * unit, step_i, (c, i)))
        events.append((first + 66 * unit, step_k, (c,)))
    events.sort(key=lambda one: one[0])

    for c in range(n):
        p0(c).start()
        for one in load_out(c):
            one.start()
    for c in range(n):
        for one in load_state(c):
            one.start()
    for _, step, args in events:
        step(*args)

    for c, (k, l, _) in enumerate(todo):
        await_(out[k].at[l, :, :, 1 - core, part(c)], a0r.at[c])
        await_(r0[k].at[l, :, :, part(c)], p0s.at[c])
        await_(out[k].at[l, :, :, 1 - core, part(c)], a0s.at[c])
        await_(r1.at[c], p1s.at[c])
        await_(r1.at[c], a1s.at[c])
        await_(r1.at[c], loc.at[c])
        await_(r3.at[c], a3s.at[c])
        for one in store_state(c):
            one.wait()

        @pl.when(outer)
        def _():
            await_(r1.at[c, :, 0], gs.at[c, 0])

        @pl.when(inner)
        def _():
            for i in range(5):
                await_(r1.at[c, :, 0], gs.at[c, i])


def solution(mesh):
    shapes = ((40, 3072), (40, 3072), (96, 1280))
    n = len(chunks())
    any_ = pl.BlockSpec(memory_space=pl.ANY)

    def step(*arrays):
        g, w, m, v = (arrays[i : i + 3] for i in (0, 3, 6, 9))
        g = [tiled(one[0], (4, 4, 2), *s) for one, s in zip(g, shapes, strict=True)]
        w = [tiled(one, (4, 4, 2), *s) for one, s in zip(w, shapes, strict=True)]
        m = [tiled(one, (), *s) for one, s in zip(m, shapes, strict=True)]
        v = [tiled(one, (), *s) for one, s in zip(v, shapes, strict=True)]
        dma = lambda *shape: pltpu.SemaphoreType.DMA(shape)
        vmem = lambda *shape, dtype=BF16: pltpu.VMEM((*shape, 8, 128), dtype)
        new = pl.pallas_call(
            kernel,
            out_shape=[jax.ShapeDtypeStruct((2, 4, 4, 2, TILES, 8, 128), BF16)] * 3
            + [jax.ShapeDtypeStruct((2, TILES, 8, 128), F32)] * 6
            + [jax.ShapeDtypeStruct((2, 4, 4, TILES, 8, 128), BF16)] * 3,
            in_specs=[any_] * 12,
            out_specs=[any_] * 12,
            scratch_shapes=[
                vmem(n, 2, 4, CUT),
                vmem(3, 2, 4, CUT),
                vmem(SLOTS, 2, 4, CUT),
                vmem(SLOTS, 2, 4, CUT),
                vmem(n, 2, 4, CUT),
                vmem(n, 5, 2, CUT),
                vmem(n, CUT),
                vmem(n, CUT),
                vmem(n, CUT, dtype=F32),
                vmem(n, CUT, dtype=F32),
                dma(n),
                dma(n),
                dma(n, 2),
                dma(3, 2),
                dma(SLOTS, 4),
                dma(n, 3),
                dma(n),
                dma(n),
                dma(n, 3),
                dma(n, 5),
                dma(n),
                dma(n),
                dma(n),
                dma(n),
                dma(n, 5),
                dma(n, 3),
                dma(n),
                dma(n),
                dma(n),
                dma(n),
                dma(n),
                dma(n, 2),
            ],
            compiler_params=pltpu.CompilerParams(has_side_effects=True, vmem_limit_bytes=67_043_328),
        )(*g, *w, *m, *v)
        shape_of = lambda i: shapes[i % 3]
        return tuple(untiled(one, *shape_of(i)) for i, one in enumerate(new[:9]))

    all_of, cut = P(None, None, None), P(None, "dp", None)
    return jax.shard_map(
        step,
        mesh=mesh,
        in_specs=(P(("rep", "dp"), None, None, None),) * 3 + (all_of,) * 3 + (cut,) * 6,
        out_specs=(P("rep", None, None),) * 3 + (P("rep", "dp", None),) * 6,
        check_vma=False,
    )
```

time: 916 us -> 431 us (0.47)
  waiting for transfers between devices: 785 us -> 0 us
  Pallas kernels: 0 us -> 391 us
  local copies, waits for them, and re-layouts: 107 us -> 39.2 us
  between operations: 14.2 us -> 0.72 us
  other arithmetic: 9.33 us -> 0.01 us
    pallas_call x0 -> x1, Pallas kernels: none -> 391 us  [step(): pl.pallas_call(kernel, out_shape=[jax.ShapeDtypeStruct((2, 4, 4, 2, TILES...]
    unnamed x8 -> x0, waiting for transfers between devices: 347 us -> none
    all_gather x3 -> x0, waiting for transfers between devices: 331 us -> none  [step(): whole = [lax.all_gather(one[0], 'dp', axis=1, tiled=True) for one in new]]
    reduce_scatter x1 -> x0, waiting for transfers between devices: 107 us -> none  [step(): lax.psum_scatter(t[0], 'dp', scatter_dimension=1, tiled=True)]
    unnamed x25 -> x31, local copies, waits for them, and re-layouts: 107 us -> 39.2 us
    convert_element_type x3 -> x0, other arithmetic: 9.33 us -> none  [adamw(): return ((w - 0.02 * step).astype(jnp.bfloat16), m, v)]
  transfers between devices with their start and end apart: 6 -> 0, of which waited for: 6 -> 0; matrix products, arithmetic and copies ran while one was open for 9% -> 0% of each run, Pallas kernels for 0% -> 0%
where the time goes in v1:
time: 431 us
  Pallas kernels  391 us (91%)
  local copies, waits for them, and re-layouts  39.2 us (9%)
    pallas_call x1, Pallas kernels, step(): pl.pallas_call(kernel, out_shape=[jax.ShapeDtypeStruct((2, 4, 4, 2, TILES...  391 us
    unnamed x31, local copies, waits for them, and re-layouts  39.2 us

profile of v1, /device:TPU:0, one launch (start us, length us, event | category | flops | bytes accessed | tf_op | source)
XLA Modules:
  0.0 430.6 jit_solution(3095231057329568970)
XLA Ops:
  0.6 390.6 %shard_map.187 = (bf16[2,4,4,2,120,8,128]{6,5,4,3,2,1,0:T(8,128)(2,1)}, bf16[2,4,4,2,120,8,128]{6,5,4,3,2,1,0:T(8,128)(2,1)}, bf16[2,4,4,2,120,8,128]{6,5,4,3,2,...) custom-call(bf16[2,4,4,2,120,8,128]{6,5,4,3,2,1,0:T(8,128)(2,1)} %bi, ...), custom_call_target="tpu_custom_call" | custom-call | tf_op jit(solution)/shard_map/pallas_call | solution.py:355
  391.3 0.0 copy-start
  391.3 0.0 slice-start
  391.3 0.0 slice-start.1
  391.3 0.0 slice-start.2
  391.3 15.9 %copy.30 = bf16[2,1280,3072]{2,1,0:T(8,128)(2,1)} copy(bf16[2,1280,3072]{2,1,0:T(8,128)(2,1)} %bitcast.115) | data formatting | bytes 31457280
  407.2 0.0 copy-done
  407.2 0.0 slice-start.3
  407.2 8.0 %copy.31 = bf16[2,1280,3072]{2,1,0:T(8,128)(2,1)} copy(bf16[2,1280,3072]{2,1,0:T(8,128)(2,1)S(1)} %bitcast.114) | data formatting | bytes 31457280
  415.2 0.0 slice-done
  415.2 0.0 slice-done.1
  415.2 1.3 slice-done.2
  416.4 1.1 slice-done.3
  417.6 0.0 copy-start.6
  417.6 0.0 copy-start.5
  417.6 0.0 copy-start.4
  417.6 0.0 copy-start.3
  417.6 0.0 copy-start.2
  417.6 0.0 copy-start.1
  417.6 7.3 %copy.32 = bf16[2,3072,1280]{2,1,0:T(8,128)(2,1)} copy(bf16[2,3072,1280]{2,1,0:T(8,128)(2,1)S(1)} %bitcast.113) | data formatting | bytes 31457280
  424.9 0.0 copy-done.6
  424.9 0.9 copy.33
  425.8 0.0 copy-done.5
  425.8 0.9 copy.34
  426.8 0.0 copy-done.4
  426.8 0.9 copy.35
  427.7 0.0 copy-done.3
  427.7 0.9 copy.36
  428.7 0.0 copy-done.2
  428.7 0.9 copy.37
  429.6 0.0 copy-done.1
  429.6 0.9 copy.38
  (1 shorter events, 0.0 us)
Async XLA Ops:
  391.3 15.9 %copy-start = (bf16[2,4,4,2,120,8,128]{6,5,4,3,2,1,0:T(8,128)(2,1)S(1)}, bf16[2,4,4,2,120,8,128]{6,5,4,3,2,1,0:T(8,128)(2,1)}, u32[]{:S(2)}) copy-start(bf16[2,4,4,2,120,8,128]{6,5,4,3,2,1,0:T(8,128)(2,1)} %get-tuple-element.19) | copy-start | bytes 47185924
  391.3 23.9 %slice-start = ((s8[15728640]{0:T(1024)(128)(4,1)}), s8[4194304]{0:T(1024)(128)(4,1)S(1)}, s32[]{:S(2)}) async-start(s8[15728640]{0:T(1024)(128)(4,1)} %bitcast.111), calls=%async_computation | async-start | bytes 8388608
  391.3 23.9 %slice-start.1 = ((s8[15728640]{0:T(1024)(128)(4,1)}), s8[4194304]{0:T(1024)(128)(4,1)S(1)}, s32[]{:S(2)}) async-start(s8[15728640]{0:T(1024)(128)(4,1)} %bitcast.111), calls=%async_computation.1 | async-start | bytes 8388608
  391.3 25.1 %slice-start.2 = ((s8[15728640]{0:T(1024)(128)(4,1)}), s8[4194304]{0:T(1024)(128)(4,1)S(1)}, s32[]{:S(2)}) async-start(s8[15728640]{0:T(1024)(128)(4,1)} %bitcast.111), calls=%async_computation.2 | async-start | bytes 8388608
  407.2 10.4 %slice-start.3 = ((s8[15728640]{0:T(1024)(128)(4,1)}), s8[3145728]{0:T(1024)(128)(4,1)S(1)}, s32[]{:S(2)}) async-start(s8[15728640]{0:T(1024)(128)(4,1)} %bitcast.111), calls=%async_computation.3 | async-start | bytes 6291456
  417.6 7.3 %copy-start.6 = (f32[2,120,8,128]{3,2,1,0:T(8,128)S(1)}, f32[2,120,8,128]{3,2,1,0:T(8,128)}, u32[]{:S(2)}) copy-start(f32[2,120,8,128]{3,2,1,0:T(8,128)} %get-tuple-element.21) | copy-start | bytes 2949124
  417.6 8.3 %copy-start.5 = (f32[2,120,8,128]{3,2,1,0:T(8,128)S(1)}, f32[2,120,8,128]{3,2,1,0:T(8,128)}, u32[]{:S(2)}) copy-start(f32[2,120,8,128]{3,2,1,0:T(8,128)} %get-tuple-element.22) | copy-start | bytes 2949124
  417.6 9.2 %copy-start.4 = (f32[2,120,8,128]{3,2,1,0:T(8,128)S(1)}, f32[2,120,8,128]{3,2,1,0:T(8,128)}, u32[]{:S(2)}) copy-start(f32[2,120,8,128]{3,2,1,0:T(8,128)} %get-tuple-element.23) | copy-start | bytes 2949124
  417.6 10.2 %copy-start.3 = (f32[2,120,8,128]{3,2,1,0:T(8,128)S(1)}, f32[2,120,8,128]{3,2,1,0:T(8,128)}, u32[]{:S(2)}) copy-start(f32[2,120,8,128]{3,2,1,0:T(8,128)} %get-tuple-element.24) | copy-start | bytes 2949124
  417.6 11.1 %copy-start.2 = (f32[2,120,8,128]{3,2,1,0:T(8,128)S(1)}, f32[2,120,8,128]{3,2,1,0:T(8,128)}, u32[]{:S(2)}) copy-start(f32[2,120,8,128]{3,2,1,0:T(8,128)} %get-tuple-element.25) | copy-start | bytes 2949124
  417.6 12.0 %copy-start.1 = (f32[2,120,8,128]{3,2,1,0:T(8,128)S(1)}, f32[2,120,8,128]{3,2,1,0:T(8,128)}, u32[]{:S(2)}) copy-start(f32[2,120,8,128]{3,2,1,0:T(8,128)} %get-tuple-element.26) | copy-start | bytes 2949124

commit v2 on v0

v2 whole, which is shorter than its diff:
```python
import functools

import jax
import jax.numpy as jnp
from jax import lax
from jax.experimental import pallas as pl
from jax.experimental.pallas import tpu as pltpu
from jax.sharding import PartitionSpec as P

TILES = 120
CUT = 60
GROUP = 12
SLOTS = 6
HOLD = 5
LIMIT_A, LIMIT_B = 31 << 20, 31 << 20
F32, BF16 = jnp.float32, jnp.bfloat16


def tiled(a, lead, rows, columns):
    a = a.reshape(2, *lead, rows // 8, 8, columns // 128, 128)
    return jnp.swapaxes(a, a.ndim - 3, a.ndim - 2).reshape(2, *lead, TILES, 8, 128)


def untiled(a, rows, columns):
    n = a.size // (2 * rows * columns)
    a = a.reshape(2, n, rows // 8, columns // 128, 8, 128)
    return jnp.swapaxes(a, 3, 4).reshape(2, n * rows, columns)


def chunks():
    return [(k, l, o) for k in range(3) for l in range(2) for o in range(0, TILES, CUT)]


def plan(n):
    tile = 2048e-3
    hop, z_rate, x_rate, b_rate, pair_rate = 1.5, 46.6e3, 90e3, 46e3, 600e3
    rank = dict(z1=0, z2=0, z3=0, z0=1, f=2, g=3, e=4, l=4, h=5, q=5.5, i=6, r=7, k=8)
    free, arrived, sent, now = {}, {}, {}, [0.0, 0.0]
    done = [{}, {}]
    pair = 4.0
    for c in range(n):
        pair += 16 * CUT * tile / pair_rate * 1e3
        arrived[0, "p0", c] = arrived[1, "p0", c] = pair + hop

    def send(p, link, blocks, rate, at, to, *name):
        start = max(at + 0.3, free.get((p, link), 0.0))
        end = start + blocks * CUT * tile / rate * 1e3 + (0.4 if link == "x" else 0.0)
        free[p, link] = end
        arrived[(to, *name)] = end + hop
        sent[(p, link, *name)] = end + hop

    def after(p, name, c, i=0):
        past = lambda *one, plus=0.0: None if one not in done[p] else done[p][one] + plus
        come = lambda *one: arrived.get((p, *one))
        if name == "l":
            return [come("p0", c)] + ([past("l", c - 1)] if c else []) + ([past("e", c - 3)] if c >= 3 else [])
        if name == "e":
            return [past("l", c, plus=1.5)]
        if name == "z0":
            return [come("p1", c), past("l", c, plus=1.5)] + ([past("r", c - SLOTS, plus=1.5)] if c >= SLOTS else [])
        if name in ("z1", "z2", "z3"):
            return [past("z0", c), come("s" + str((0, 1, 3)[int(name[1]) - 1]), c)]
        if name == "f":
            if p == 0:
                return [past("z0", c), come("s3", c)]
            return [past("z1", c), past("z2", c), past("z3", c), come("s2", c), come("s4", c)]
        if name == "g":
            return [past("f", c), come("p3", c)]
        if name == "h":
            return [past("g", c), come("a3", c)]
        if name == "q":
            return [past("h", c)] + ([past("z0", min(n - 1, c + HOLD))] if p == 0 else [])
        if name == "r":
            if p == 0:
                sends = [sent.get((p, "in", "s" + str(j), c)) for j in range(3)]
            else:
                sends = [sent.get((p, *one, c)) for one in (("in", "s3"), ("in", "s4"), ("out", "s3"))]
            return [past("g", c), sent.get((p, "b", "p3", c)), *sends]
        if name == "i":
            return [past("q", c), come("n" + str(i), c)] + ([past("i", c, i - 1)] if i else [])
        return [past("i", c, 2), come("a1", c)]

    def run(p, at, name, c, i=0):
        work = CUT * 0.004
        if name == "e":
            at += 6 * work + 0.3
            send(p, "x", 8, x_rate, at, p, "p1", c)
        elif name == "z0" and p == 0:
            for j in range(3):
                at += 2 * work + 0.1
                send(p, "in", 2, z_rate, at, 1, "s" + str(j), c)
        elif name in ("z1", "z2"):
            at += 2 * work + 0.1
            send(p, "in", 2, z_rate, at, 1, "s3" if name == "z1" else "s4", c)
        elif name == "z3":
            at += 2 * work + 0.1
            send(p, "out", 2, z_rate, at, 0, "s3", c)
        elif name == "f":
            at += 1.3 * work + 0.1
            send(p, "b", 1, b_rate, at, p, "p3", c)
        elif name == "g":
            at += 4 * work + 0.2
            send(p, "b", 1, b_rate, at, p, "a3", c)
        elif name == "q":
            at += 0.1
            if p == 0:
                send(p, "in", 2, z_rate, at, 1, "n0", c)
            else:
                send(p, "out", 2, z_rate, at, 0, "n0", c)
                send(p, "in", 2, z_rate, at, 1, "n1", c)
        elif name == "i":
            at += 0.3
            if p == 1 and i == 0:
                send(p, "in", 2, z_rate, at, 1, "n2", c)
            elif p == 1:
                send(p, "out", 2, z_rate, at, 0, "n" + str(i), c)
            if i != 1:
                send(p, "x", 4, x_rate, at, p, "a1" if i else "a1 first", c)
        else:
            at += 0.3
        return at

    both = ("l", "e", "z0", "f", "g", "h", "q", "r", "k")
    left = [[(name, c) for c in range(n) for name in both] + [("i", c, i) for c in range(n) for i in range(3)] for _ in range(2)]
    left[1] += [(name, c) for c in range(n) for name in ("z1", "z2", "z3")]
    order = [[], []]
    while left[0] or left[1]:
        best = None
        for p in range(2):
            for one in left[p]:
                times = after(p, *one)
                if None not in times:
                    key = (max(now[p], *times), rank[one[0]], one[1], p, one)
                    best = key if best is None or key < best else best
        at, _, _, p, one = best
        left[p].remove(one)
        now[p] = done[p][one] = run(p, at, *one)
        order[p].append(one)
    return order


def kernel(*refs):
    g, w, m, v = (refs[i : i + 3] for i in (0, 3, 6, 9))
    out, r0, (r1, po, mb, vb) = refs[12:15], refs[15:18], refs[18:22]
    t0, kg, kr, r2, r3, wb = refs[22:28]
    (p0s, p0r, lg, lt, lk, lm, p1s, p1r, zs, zr, p3s, p3r, a3s, a3r, gs, gr, a1s, a1r, a0s, a0r, credit) = refs[28:]
    todo = chunks()
    n = len(todo)

    me = lax.axis_index("dp")
    core, z, y, x = me % 2, me // 2 % 4, me // 8 % 2, me // 16
    a, b = x * (1 - core) + y * core, y * (1 - core) + x * core
    sa, sb = 2 - core, 1 + core
    far = z // 2
    turn = 1 - 2 * far
    here = z * turn + 3 * far
    partner = me + 1 - 2 * core
    beside_a = ((1 - a) * sa + b * sb) * 8 + z * 2 + core
    beside_b = (a * sa + (1 - b) * sb) * 8 + z * 2 + core
    inward, outward = me + 2 * turn, me - 2 * turn

    def xy(one_a, one_b):
        return one_a * sa + one_b * sb

    def along(t):
        return t * turn + 3 * far

    def remote(src, dst, send, recv, device):
        return pltpu.make_async_remote_copy(
            src_ref=src, dst_ref=dst, send_sem=send, recv_sem=recv, device_id={"dp": device}, device_id_type=pl.DeviceIdType.MESH
        )

    def await_(ref, sem):
        pltpu.make_async_copy(ref, ref, sem).wait()

    def part(c):
        return pl.ds(todo[c][2], CUT)

    def add(dst, *terms):
        @pl.loop(0, CUT // GROUP)
        def _(i):
            at = pl.ds(i * GROUP, GROUP)
            total = terms[0][at].astype(F32)
            for term in terms[1:]:
                total = total + term[at].astype(F32)
            dst[at] = total.astype(BF16)

    def p0(c):
        k, l, _ = todo[c]
        return remote(g[k].at[l, :, :, 1 - core, part(c)], r0[k].at[l, :, :, part(c)], p0s.at[c], p0r.at[c], partner)

    def load_out(c):
        k, l, _ = todo[c]
        return [pltpu.make_async_copy(g[k].at[l, xy(1 - a, j), :, core, part(c)], po.at[c, j], lg.at[c, j]) for j in range(2)]

    def load_out_r0(c):
        k, l, _ = todo[c]
        return [pltpu.make_async_copy(r0[k].at[l, xy(1 - a, j), :, part(c)], t0.at[c % 3, j], lt.at[c % 3, j]) for j in range(2)]

    def load_kept(c):
        k, l, _ = todo[c]
        s = c % SLOTS
        return [pltpu.make_async_copy(g[k].at[l, xy(a, j), :, core, part(c)], kg.at[s, j], lk.at[s, j]) for j in range(2)] + [
            pltpu.make_async_copy(r0[k].at[l, xy(a, j), :, part(c)], kr.at[s, j], lk.at[s, 2 + j]) for j in range(2)
        ]

    def load_state(c):
        k, l, _ = todo[c]
        return [
            pltpu.make_async_copy(w[k].at[l, x * 2 + y, z, core, part(c)], wb.at[c], lm.at[c, 0]),
            pltpu.make_async_copy(m[k].at[l, part(c)], mb.at[c], lm.at[c, 1]),
            pltpu.make_async_copy(v[k].at[l, part(c)], vb.at[c], lm.at[c, 2]),
        ]

    def p1(c):
        return remote(po.at[c], r1.at[c], p1s.at[c], p1r.at[c], beside_a)

    def zsend(c, i, t, slot, device):
        return remote(kg.at[c % SLOTS, :, along(t)], r2.at[c, slot], zs.at[c, i], zr.at[c, slot], device)

    def p3(c):
        return remote(kg.at[c % SLOTS, 1 - b, z], r3.at[c], p3s.at[c], p3r.at[c], beside_b)

    def a3(c):
        return remote(r1.at[c, b, z], r1.at[c, b, z], a3s.at[c], a3r.at[c], beside_b)

    def gsend(c, i, t, slot, device):
        where = r1.at[c, :, along(t)]
        return remote(where, where, gs.at[c, i], gr.at[c, slot], device)

    def a1(c, half):
        at = pl.ds(2 * far + 2 * half * turn, 2)
        return remote(r1.at[c, :, at], po.at[c, :, at], a1s.at[c, half], a1r.at[c, half], beside_a)

    def a0(c, mine):
        k, l, _ = todo[c]
        src = r1 if mine else po
        return [
            remote(src.at[c, j], out[k].at[l, xy(a if mine else 1 - a, j), :, part(c)], a0s.at[c], a0r.at[c], partner) for j in range(2)
        ]

    def kept_terms(c, j, t, *slots):
        s = c % SLOTS
        return (kg.at[s, j, t], kr.at[s, j, t], r1.at[c, j, t], *(r2.at[c, i, j] for i in slots))

    def sum_piece(c, t, *slots):
        for j in range(2):
            add(kg.at[c % SLOTS, j, along(t)], *kept_terms(c, j, along(t), *slots))

    def steps(end):
        freed, ready = set(range(SLOTS)), set()

        def maybe_load(c):
            if c in freed and c in ready:
                for one in load_kept(c):
                    one.start()

        last = (3,) if end else (2, 4)

        def step_l(c):
            await_(r0[todo[c][0]].at[todo[c][1], :, :, part(c)], p0r.at[c])
            for one in load_out_r0(c):
                one.start()
            ready.add(c)
            maybe_load(c)

        def step_e(c):
            for one in load_out(c) + load_out_r0(c):
                one.wait()

            @pl.loop(0, 8)
            def _(i):
                add(po.at[c, i // 4, i % 4], po.at[c, i // 4, i % 4], t0.at[c % 3, i // 4, i % 4])

            p1(c).start()

        def step_z0(c):
            for one in load_kept(c):
                one.wait()
            await_(r1.at[c], p1r.at[c])
            await_(po.at[c], p1s.at[c])
            pl.semaphore_signal(credit.at[c], inc=1, device_id={"dp": beside_a}, device_id_type=pl.DeviceIdType.MESH)
            if end:
                for i, t in enumerate((3, 2, 1)):
                    sum_piece(c, t)
                    zsend(c, i, t, i, inward).start()

        def step_z1(c):
            await_(r2.at[c, 0], zr.at[c, 0])
            sum_piece(c, 3, 0)
            zsend(c, 0, 3, 3, inward).start()

        def step_z2(c):
            await_(r2.at[c, 1], zr.at[c, 1])
            sum_piece(c, 2, 1)
            zsend(c, 1, 2, 4, inward).start()

        def step_z3(c):
            await_(r2.at[c, 3], zr.at[c, 3])
            sum_piece(c, 0, 3)
            zsend(c, 2, 0, 3, outward).start()

        def step_f(c):
            for i in last:
                await_(r2.at[c, i], zr.at[c, i])
            add(kg.at[c % SLOTS, 1 - b, z], *kept_terms(c, 1 - b, z, *last))
            p3(c).start()

        def step_g(c):
            await_(r3.at[c], p3r.at[c])
            for one in load_state(c):
                one.wait()
            terms = (*kept_terms(c, b, z, *last), r3.at[c])

            @pl.loop(0, CUT // GROUP)
            def _(i):
                at = pl.ds(i * GROUP, GROUP)
                total = terms[0][at].astype(F32)
                for term in terms[1:]:
                    total = total + term[at].astype(F32)
                grad = total.astype(BF16).astype(F32)
                one_m = 0.9 * mb[c, at] + 0.1 * grad
                one_v = 0.95 * vb[c, at] + 0.05 * grad * grad
                one_w = wb[c, at].astype(F32)
                mb[c, at] = one_m
                vb[c, at] = one_v
                r1[c, b, z, at] = (one_w - 0.02 * (one_m * lax.rsqrt(one_v + 1e-8) + 0.1 * one_w)).astype(BF16)

            a3(c).start()

        def step_h(c):
            await_(r1.at[c, 1 - b, z], a3r.at[c])

        def step_q(c):
            if end:
                gsend(c, 0, 0, 0, inward).start()
            else:
                gsend(c, 0, 1, 0, outward).start()
                gsend(c, 1, 1, 1, inward).start()

        def step_r(c):
            for i in range(3):
                await_(kg.at[c % SLOTS, :, 0], zs.at[c, i])
            await_(r3.at[c], p3s.at[c])
            freed.add(c + SLOTS)
            maybe_load(c + SLOTS)

        def step_i(c, i):
            t = i + 1 if end else (0, 2, 3)[i]
            await_(r1.at[c, :, along(t)], gr.at[c, i])
            if not end and i == 0:
                gsend(c, 2, 0, 2, inward).start()
            elif not end:
                gsend(c, 2 + i, t, i, outward).start()
            if i == 0:
                pl.semaphore_wait(credit.at[c], 1)
                a1(c, 0).start()
            elif i == 2:
                a1(c, 1).start()
                for one in a0(c, True):
                    one.start()

        def step_k(c):
            for half in range(2):
                await_(r1.at[c, :, :2], a1r.at[c, half])
            for one in a0(c, False):
                one.start()

        return dict(
            l=step_l, e=step_e, z0=step_z0, z1=step_z1, z2=step_z2, z3=step_z3, f=step_f,
            g=step_g, h=step_h, q=step_q, r=step_r, i=step_i, k=step_k,
        )

    for c in range(n):
        p0(c).start()
        for one in load_out(c):
            one.start()
    for c in range(n):
        for one in load_state(c):
            one.start()

    order = plan(n)

    @pl.when(here == 0)
    def _():
        take = steps(True)
        for name, *args in order[0]:
            take[name](*args)
        for c in range(n):
            await_(r1.at[c, :, 0], gs.at[c, 0])

    @pl.when(here == 1)
    def _():
        take = steps(False)
        for name, *args in order[1]:
            take[name](*args)
        for c in range(n):
            for i in range(5):
                await_(r1.at[c, :, 0], gs.at[c, i])

    for c, (k, l, _) in enumerate(todo):
        await_(out[k].at[l, :, :, part(c)], a0r.at[c])
        await_(out[k].at[l, :, :, part(c)], a0s.at[c])
        await_(r0[k].at[l, :, :, part(c)], p0s.at[c])
        for half in range(2):
            await_(r1.at[c, :, :2], a1s.at[c, half])
        await_(r3.at[c], a3s.at[c])


def finish(*refs):
    r1, po, mb, vb, *other = refs[:7]
    new_w, new_m, new_v = (refs[i : i + 3] for i in (7, 10, 13))
    buf, here, there, state, ls, ss = refs[16:]
    todo = chunks()
    me = lax.axis_index("dp")
    core, y, x = me % 2, me // 8 % 2, me // 16
    a = x * (1 - core) + y * core
    sa, sb = 2 - core, 1 + core
    copies = []

    def load(c):
        k, l, o = todo[c]
        return pltpu.make_async_copy(other[k].at[l, :, :, pl.ds(o, CUT)], buf.at[c], ls.at[c])

    for c in range(len(todo)):
        load(c).start()
    for c, (k, l, o) in enumerate(todo):
        at = pl.ds(o, CUT)
        for j in range(2):
            copies.append(pltpu.make_async_copy(r1.at[c, j], new_w[k].at[l, a * sa + j * sb, :, core, at], here.at[c, j]))
            copies.append(pltpu.make_async_copy(po.at[c, j], new_w[k].at[l, (1 - a) * sa + j * sb, :, core, at], there.at[c, j]))
        copies.append(pltpu.make_async_copy(mb.at[c], new_m[k].at[l, at], state.at[c, 0]))
        copies.append(pltpu.make_async_copy(vb.at[c], new_v[k].at[l, at], state.at[c, 1]))
    for one in copies:
        one.start()
    for c, (k, l, o) in enumerate(todo):
        load(c).wait()
        one = pltpu.make_async_copy(buf.at[c], new_w[k].at[l, :, :, 1 - core, pl.ds(o, CUT)], ss.at[c])
        one.start()
        copies.append(one)
    for one in copies:
        one.wait()


def solution(mesh):
    shapes = ((40, 3072), (40, 3072), (96, 1280))
    n = len(chunks())
    any_ = pl.BlockSpec(memory_space=pl.ANY)

    def step(*arrays):
        g, w, m, v = (arrays[i : i + 3] for i in (0, 3, 6, 9))
        g = [tiled(one[0], (4, 4, 2), *s) for one, s in zip(g, shapes, strict=True)]
        w = [tiled(one, (4, 4, 2), *s) for one, s in zip(w, shapes, strict=True)]
        m = [tiled(one, (), *s) for one, s in zip(m, shapes, strict=True)]
        v = [tiled(one, (), *s) for one, s in zip(v, shapes, strict=True)]
        dma = lambda *shape: pltpu.SemaphoreType.DMA(shape)
        vmem = lambda *shape, dtype=BF16: pltpu.VMEM((*shape, 8, 128), dtype)
        shape = lambda *shape, dtype=BF16: jax.ShapeDtypeStruct((*shape, 8, 128), dtype)
        on_chip, off_chip = pl.BlockSpec(memory_space=pltpu.VMEM), pl.BlockSpec(memory_space=pltpu.HBM)
        keep = pltpu.with_memory_space_constraint
        *other, _, _, _, r1, po, mb, vb = pl.pallas_call(
            kernel,
            out_shape=[pltpu.HBM((2, 4, 4, TILES, 8, 128), BF16)] * 6 + [vmem(n, 2, 4, CUT)] * 2 + [vmem(n, CUT, dtype=F32)] * 2,
            in_specs=[any_] * 12,
            out_specs=[off_chip] * 6 + [on_chip] * 4,
            scratch_shapes=[
                vmem(3, 2, 4, CUT),
                vmem(SLOTS, 2, 4, CUT),
                vmem(SLOTS, 2, 4, CUT),
                vmem(n, 5, 2, CUT),
                vmem(n, CUT),
                vmem(n, CUT),
                dma(n),
                dma(n),
                dma(n, 2),
                dma(3, 2),
                dma(SLOTS, 4),
                dma(n, 3),
                dma(n),
                dma(n),
                dma(n, 3),
                dma(n, 5),
                dma(n),
                dma(n),
                dma(n),
                dma(n),
                dma(n, 5),
                dma(n, 3),
                dma(n, 2),
                dma(n, 2),
                dma(n),
                dma(n),
                pltpu.SemaphoreType.REGULAR((n,)),
            ],
            compiler_params=pltpu.CompilerParams(has_side_effects=True, vmem_limit_bytes=LIMIT_A),
        )(*g, *w, *m, *v)
        new = pl.pallas_call(
            finish,
            out_shape=[shape(2, 4, 4, 2, TILES)] * 3 + [shape(2, TILES, dtype=F32)] * 6,
            in_specs=[on_chip] * 4 + [off_chip] * 3,
            out_specs=[any_] * 9,
            scratch_shapes=[vmem(n, 4, 4, CUT), dma(n, 2), dma(n, 2), dma(n, 2), dma(n), dma(n)],
            compiler_params=pltpu.CompilerParams(vmem_limit_bytes=LIMIT_B),
        )(*(keep(one, pltpu.VMEM) for one in (r1, po, mb, vb)), *(keep(one, pltpu.HBM) for one in other))
        shape_of = lambda i: shapes[i % 3]
        return tuple(untiled(one, *shape_of(i)) for i, one in enumerate(new))

    all_of, cut = P(None, None, None), P(None, "dp", None)
    return jax.shard_map(
        step,
        mesh=mesh,
        in_specs=(P(("rep", "dp"), None, None, None),) * 3 + (all_of,) * 3 + (cut,) * 6,
        out_specs=(P("rep", None, None),) * 3 + (P("rep", "dp", None),) * 6,
        check_vma=False,
    )
```

time: 916 us -> 382 us (0.42)
  waiting for transfers between devices: 785 us -> 0 us
  Pallas kernels: 0 us -> 380 us
  local copies, waits for them, and re-layouts: 107 us -> 0 us
  between operations: 14.2 us -> 0.65 us
  other arithmetic: 9.33 us -> 0 us
    pallas_call x0 -> x2, Pallas kernels: none -> 380 us  [the longest x1 355 us: step(): pl.pallas_call(kernel, out_shape=[pltpu.HBM((2, 4, 4, TILES, 8, 128), BF1...]
    unnamed x8 -> x0, waiting for transfers between devices: 347 us -> none
    all_gather x3 -> x0, waiting for transfers between devices: 331 us -> none  [step(): whole = [lax.all_gather(one[0], 'dp', axis=1, tiled=True) for one in new]]
    unnamed x25 -> x0, local copies, waits for them, and re-layouts: 107 us -> none
    reduce_scatter x1 -> x0, waiting for transfers between devices: 107 us -> none  [step(): lax.psum_scatter(t[0], 'dp', scatter_dimension=1, tiled=True)]
    convert_element_type x3 -> x0, other arithmetic: 9.33 us -> none  [adamw(): return ((w - 0.02 * step).astype(jnp.bfloat16), m, v)]
  transfers between devices with their start and end apart: 6 -> 0, of which waited for: 6 -> 0; matrix products, arithmetic and copies ran while one was open for 9% -> 0% of each run, Pallas kernels for 0% -> 0%
where the time goes in v2:
time: 382 us; the launch traced here: 381 us
  Pallas kernels  380 us (99%)
    pallas_call x1, Pallas kernels, step(): pl.pallas_call(kernel, out_shape=[pltpu.HBM((2, 4, 4, TILES, 8, 128), BF1...  355 us
    pallas_call x1, Pallas kernels, step(): pl.pallas_call(finish, out_shape=[shape(2, 4, 4, 2, TILES)] * 3 + [shape(...  25.9 us

profile of v2, /device:TPU:0, one launch (start us, length us, event | category | flops | bytes accessed | tf_op | source)
XLA Modules:
  0.0 381.1 jit_solution(5360536066151428899)
XLA Ops:
  0.6 354.5 %shard_map.187 = (bf16[2,4,4,120,8,128]{5,4,3,2,1,0:T(8,128)(2,1)}, bf16[2,4,4,120,8,128]{5,4,3,2,1,0:T(8,128)(2,1)}, bf16[2,4,4,120,8,128]{5,4,3,2,1,0:T(8,128)...) custom-call(bf16[2,4,4,2,120,8,128]{6,5,4,3,2,1,0:T(8,128)(2,1)} %bi, ...), custom_call_target="tpu_custom_call" | custom-call | tf_op jit(solution)/shard_map/pallas_call | solution.py:461
  355.2 25.9 %shard_map.188 = (bf16[2,4,4,2,120,8,128]{6,5,4,3,2,1,0:T(8,128)(2,1)}, bf16[2,4,4,2,120,8,128]{6,5,4,3,2,1,0:T(8,128)(2,1)}, bf16[2,4,4,2,120,8,128]{6,5,4,3,2,...) custom-call(bf16[12,2,4,60,8,128]{5,4,3,2,1,0:T(8,128)(2,1)S(1)} %ge, ...), custom_call_target="tpu_custom_call" | custom-call | tf_op jit(solution)/shard_map/pallas_call | solution.py:497

commit v3 on v2

v3 whole, which is shorter than its diff:
```python
import functools

import jax
import jax.numpy as jnp
from jax import lax
from jax.experimental import pallas as pl
from jax.experimental.pallas import tpu as pltpu
from jax.sharding import PartitionSpec as P

TILES = 120
CUT = 40
GROUP = 20
SLOTS = 9
HOLD = 6
LIMIT = 9 << 20
F32, BF16 = jnp.float32, jnp.bfloat16


def tiled(a, lead, rows, columns):
    a = a.reshape(2, *lead, rows // 8, 8, columns // 128, 128)
    return jnp.swapaxes(a, a.ndim - 3, a.ndim - 2).reshape(2, *lead, TILES, 8, 128)


def untiled(a, rows, columns):
    n = a.size // (2 * rows * columns)
    a = a.reshape(2, n, rows // 8, columns // 128, 8, 128)
    return jnp.swapaxes(a, 3, 4).reshape(2, n * rows, columns)


def chunks():
    return [(k, l, o) for k in range(3) for l in range(2) for o in range(0, TILES, CUT)]


def plan(n):
    tile = 2048e-3
    hop, z_rate, x_rate, b_rate, pair_rate = 1.5, 46.6e3, 90e3, 46e3, 600e3
    rank = dict(z1=0, z2=0, z3=0, z0=1, f=2, g=3, e=4, l=4, h=5, q=5.5, i=6, r=7, k=8, w=9)
    free, arrived, sent, now = {}, {}, {}, [0.0, 0.0]
    done = [{}, {}]
    pair = 4.0
    for c in range(n):
        pair += 16 * CUT * tile / pair_rate * 1e3
        arrived[0, "p0", c] = arrived[1, "p0", c] = pair + hop

    def send(p, link, blocks, rate, at, to, *name):
        start = max(at + 0.3, free.get((p, link), 0.0))
        end = start + blocks * CUT * tile / rate * 1e3 + (0.4 if link == "x" else 0.0)
        free[p, link] = end
        arrived[(to, *name)] = end + hop
        sent[(p, link, *name)] = end + hop

    def after(p, name, c, i=0):
        past = lambda *one, plus=0.0: None if one not in done[p] else done[p][one] + plus
        come = lambda *one: arrived.get((p, *one))
        if name == "l":
            return [come("p0", c)] + ([past("l", c - 1)] if c else []) + ([past("e", c - 3)] if c >= 3 else [])
        if name == "e":
            return [past("l", c, plus=1.5)]
        if name == "z0":
            return [come("p1", c), past("l", c, plus=1.5)] + ([past("r", c - SLOTS, plus=1.5)] if c >= SLOTS else [])
        if name in ("z1", "z2", "z3"):
            return [past("z0", c), come("s" + str((0, 1, 3)[int(name[1]) - 1]), c)]
        if name == "f":
            if p == 0:
                return [past("z0", c), come("s3", c)]
            return [past("z1", c), past("z2", c), past("z3", c), come("s2", c), come("s4", c)]
        if name == "g":
            return [past("f", c), come("p3", c)]
        if name == "h":
            return [past("g", c), come("a3", c)]
        if name == "q":
            return [past("h", c)] + ([past("z0", min(n - 1, c + HOLD))] if p == 0 else [])
        if name == "r":
            if p == 0:
                sends = [sent.get((p, "in", "s" + str(j), c)) for j in range(3)]
            else:
                sends = [sent.get((p, *one, c)) for one in (("in", "s3"), ("in", "s4"), ("out", "s3"))]
            return [past("g", c), sent.get((p, "b", "p3", c)), *sends]
        if name == "i":
            return [past("q", c), come("n" + str(i), c)] + ([past("i", c, i - 1)] if i else [])
        if name == "k":
            return [past("i", c, 2), come("a1", c)]
        return [past("k", c), come("a0", c)] + [past("r", j) for j in range(n)]

    def run(p, at, name, c, i=0):
        work = CUT * 0.004
        if name == "e":
            at += 6 * work + 0.3
            send(p, "x", 8, x_rate, at, p, "p1", c)
        elif name == "z0" and p == 0:
            for j in range(3):
                at += 2 * work + 0.1
                send(p, "in", 2, z_rate, at, 1, "s" + str(j), c)
        elif name in ("z1", "z2"):
            at += 2 * work + 0.1
            send(p, "in", 2, z_rate, at, 1, "s3" if name == "z1" else "s4", c)
        elif name == "z3":
            at += 2 * work + 0.1
            send(p, "out", 2, z_rate, at, 0, "s3", c)
        elif name == "f":
            at += 1.3 * work + 0.1
            send(p, "b", 1, b_rate, at, p, "p3", c)
        elif name == "g":
            at += 4 * work + 0.2
            send(p, "b", 1, b_rate, at, p, "a3", c)
        elif name == "q":
            at += 0.1
            if p == 0:
                send(p, "in", 2, z_rate, at, 1, "n0", c)
            else:
                send(p, "out", 2, z_rate, at, 0, "n0", c)
                send(p, "in", 2, z_rate, at, 1, "n1", c)
        elif name == "i":
            at += 0.3
            if p == 1 and i == 0:
                send(p, "in", 2, z_rate, at, 1, "n2", c)
            elif p == 1:
                send(p, "out", 2, z_rate, at, 0, "n" + str(i), c)
            if i != 1:
                send(p, "x", 4, x_rate, at, p, "a1" if i else "a1 first", c)
        else:
            at += 0.3
            if name == "k":
                send(p, "d", 8, pair_rate, at, p, "a0", c)
        return at

    both = ("l", "e", "z0", "f", "g", "h", "q", "r", "k", "w")
    left = [[(name, c) for c in range(n) for name in both] + [("i", c, i) for c in range(n) for i in range(3)] for _ in range(2)]
    left[1] += [(name, c) for c in range(n) for name in ("z1", "z2", "z3")]
    order = [[], []]
    while left[0] or left[1]:
        best = None
        for p in range(2):
            for one in left[p]:
                times = after(p, *one)
                if None not in times:
                    key = (max(now[p], *times), rank[one[0]], one[1], p, one)
                    best = key if best is None or key < best else best
        at, _, _, p, one = best
        left[p].remove(one)
        now[p] = done[p][one] = run(p, at, *one)
        order[p].append(one)
    return order


def kernel(*refs):
    g, w, m, v = (refs[i : i + 3] for i in (0, 3, 6, 9))
    out, r0, (r1, po, ph, mb, vb) = refs[12:15], refs[15:18], refs[18:23]
    t0, r2, r3, wb = refs[23:27]
    p0s, p0r, lo, lk, lw, lm, p1s, p1r, ks, zr, p3r, a3s, a3r, gs, gr, a1s, a1r, a0s, a0r, lp, credit = refs[27:]
    todo = chunks()
    n = len(todo)

    me = lax.axis_index("dp")
    core, z, y, x = me % 2, me // 2 % 4, me // 8 % 2, me // 16
    a, b = x * (1 - core) + y * core, y * (1 - core) + x * core
    sa, sb = 2 - core, 1 + core
    far = z // 2
    turn = 1 - 2 * far
    here = z * turn + 3 * far
    partner = me + 1 - 2 * core
    beside_a = ((1 - a) * sa + b * sb) * 8 + z * 2 + core
    beside_b = (a * sa + (1 - b) * sb) * 8 + z * 2 + core
    inward, outward = me + 2 * turn, me - 2 * turn

    own_xy, other_xy = [a * sa, a * sa + sb], [(1 - a) * sa, (1 - a) * sa + sb]
    line = [t * turn + 3 * far for t in range(4)]
    halves = [pl.ds(2 * far, 2), pl.ds(2 * far + 2 * turn, 2)]
    not_core, not_b, state_xy = 1 - core, 1 - b, x * 2 + y

    def remote(src, dst, send, recv, device):
        return pltpu.make_async_remote_copy(
            src_ref=src, dst_ref=dst, send_sem=send, recv_sem=recv, device_id={"dp": device}, device_id_type=pl.DeviceIdType.MESH
        )

    def await_(ref, sem):
        pltpu.make_async_copy(ref, ref, sem).wait()

    def part(c):
        return pl.ds(todo[c][2], CUT)

    def kept(c, j, t):
        return ph.at[2 * (c % SLOTS), t, 2 + j]

    def kept_r0(c, j, t):
        return ph.at[2 * (c % SLOTS) + 1, t, 2 + j]

    def piece(c, t):
        return ph.at[2 * (c % SLOTS), t, pl.ds(2, 2)]

    def slot(c, i):
        return ph.at[c, i, pl.ds(0, 2)] if i < 4 else r2.at[c]

    def total(i, terms):
        value = terms[0][i].astype(F32)
        for term in terms[1:]:
            value = value + term[i].astype(F32)
        return value.astype(BF16)

    def add(dst, *terms):
        @pl.loop(0, CUT // GROUP)
        def _(i):
            at = pl.ds(i * GROUP, GROUP)
            dst[at] = total(at, terms)

    def p0(c):
        k, l, _ = todo[c]
        return remote(g[k].at[l, :, :, not_core, part(c)], r0[k].at[l, :, :, part(c)], p0s.at[c], p0r.at[c], partner)

    def load_out(c):
        k, l, _ = todo[c]
        return [pltpu.make_async_copy(g[k].at[l, other_xy[j], :, core, part(c)], po.at[c, j], lo.at[c]) for j in range(2)]

    def load_out_r0(c):
        k, l, _ = todo[c]
        return [pltpu.make_async_copy(r0[k].at[l, other_xy[j], :, part(c)], t0.at[c % 3, j], lo.at[c]) for j in range(2)]

    def load_kept(c):
        k, l, _ = todo[c]
        s = c % SLOTS
        return [pltpu.make_async_copy(g[k].at[l, own_xy[j], :, core, part(c)], ph.at[2 * s, :, 2 + j], lk.at[s]) for j in range(2)] + [
            pltpu.make_async_copy(r0[k].at[l, own_xy[j], :, part(c)], ph.at[2 * s + 1, :, 2 + j], lk.at[s]) for j in range(2)
        ]

    def load_state(c):
        k, l, _ = todo[c]
        return [
            pltpu.make_async_copy(w[k].at[l, state_xy, z, core, part(c)], wb.at[c], lw.at[c]),
            pltpu.make_async_copy(m[k].at[l, part(c)], mb.at[c], lm.at[c]),
            pltpu.make_async_copy(v[k].at[l, part(c)], vb.at[c], lm.at[c]),
        ]

    def p1(c):
        return remote(po.at[c], r1.at[c], p1s.at[c], p1r.at[c], beside_a)

    def zsend(c, t, i, device):
        return remote(piece(c, line[t]), slot(c, i), ks.at[c], zr.at[c, i], device)

    def p3(c):
        return remote(kept(c, not_b, z), r3.at[c], ks.at[c], p3r.at[c], beside_b)

    def a3(c):
        return remote(r1.at[c, b, z], r1.at[c, b, z], a3s.at[c], a3r.at[c], beside_b)

    def gsend(c, t, i, device):
        where = r1.at[c, :, line[t]]
        return remote(where, where, gs.at[c], gr.at[c, i], device)

    def a1(c, half):
        at = halves[half]
        return remote(r1.at[c, :, at], po.at[c, :, at], a1s.at[c], a1r.at[c], beside_a)

    def a0(c, mine):
        k, l, _ = todo[c]
        src = r1 if mine else po
        return [
            remote(src.at[c, j], out[k].at[l, (own_xy if mine else other_xy)[j], :, part(c)], a0s.at[c], a0r.at[c], partner) for j in range(2)
        ]

    def sum_piece(c, t, *slots):
        t = line[t]

        @pl.loop(0, 2)
        def _(j):
            add(kept(c, j, t), kept(c, j, t), kept_r0(c, j, t), r1.at[c, j, t], *(slot(c, i).at[j] for i in slots))

    def steps(end):
        freed, ready = set(range(SLOTS)), set()

        def maybe_load(c):
            if c in freed and c in ready:
                for one in load_kept(c):
                    one.start()

        last = (3,) if end else (2, 4)

        def step_l(c):
            await_(r0[todo[c][0]].at[todo[c][1], :, :, part(c)], p0r.at[c])
            for one in load_out_r0(c):
                one.start()
            ready.add(c)
            maybe_load(c)

        def step_e(c):
            await_(t0.at[:2], lo.at[c])

            for j in range(2):

                @pl.loop(0, 4)
                def _(t, j=j):
                    add(po.at[c, j, t], po.at[c, j, t], t0.at[c % 3, j, t])

            p1(c).start()

        def step_z0(c):
            await_(t0.at[:2], lk.at[c % SLOTS])
            await_(r1.at[c], p1r.at[c])
            await_(po.at[c], p1s.at[c])
            pl.semaphore_signal(credit.at[c], inc=1, device_id={"dp": beside_a}, device_id_type=pl.DeviceIdType.MESH)
            if end:
                for i, t in enumerate((3, 2, 1)):
                    sum_piece(c, t)
                    zsend(c, t, i, inward).start()

        def step_z1(c):
            await_(slot(c, 0), zr.at[c, 0])
            sum_piece(c, 3, 0)
            zsend(c, 3, 3, inward).start()

        def step_z2(c):
            await_(slot(c, 1), zr.at[c, 1])
            sum_piece(c, 2, 1)
            zsend(c, 2, 4, inward).start()

        def step_z3(c):
            await_(slot(c, 3), zr.at[c, 3])
            sum_piece(c, 0, 3)
            zsend(c, 0, 3, outward).start()

        def own_terms(c, j):
            return [kept(c, j, z), kept_r0(c, j, z), r1.at[c, j, z], *(slot(c, i).at[j] for i in last)]

        def step_f(c):
            for i in last:
                await_(slot(c, i), zr.at[c, i])
            add(kept(c, not_b, z), *own_terms(c, not_b))
            p3(c).start()

        def step_g(c):
            await_(r3.at[c], p3r.at[c])
            await_(wb.at[c], lw.at[c])
            await_(mb.at[:2], lm.at[c])

            @pl.loop(0, CUT // GROUP)
            def _(i):
                at = pl.ds(i * GROUP, GROUP)
                grad = total(at, [*own_terms(c, b), r3.at[c]]).astype(F32)
                one_m = 0.9 * mb[c, at] + 0.1 * grad
                one_v = 0.95 * vb[c, at] + 0.05 * grad * grad
                one_w = wb[c, at].astype(F32)
                mb[c, at] = one_m
                vb[c, at] = one_v
                r1[c, b, z, at] = (one_w - 0.02 * (one_m * lax.rsqrt(one_v + 1e-8) + 0.1 * one_w)).astype(BF16)

            a3(c).start()

        def step_h(c):
            await_(r1.at[c, not_b, z], a3r.at[c])

        def step_q(c):
            if end:
                gsend(c, 0, 0, inward).start()
            else:
                gsend(c, 1, 0, outward).start()
                gsend(c, 1, 1, inward).start()

        def step_r(c):
            await_(r3.at[:7], ks.at[c])
            freed.add(c + SLOTS)
            maybe_load(c + SLOTS)

        def step_i(c, i):
            t = i + 1 if end else (0, 2, 3)[i]
            await_(r1.at[c, :, line[t]], gr.at[c, i])
            if not end and i == 0:
                gsend(c, 0, 2, inward).start()
            elif not end:
                gsend(c, t, i, outward).start()
            if i == 0:
                pl.semaphore_wait(credit.at[c], 1)
                a1(c, 0).start()
            elif i == 2:
                a1(c, 1).start()
                for one in a0(c, True):
                    one.start()

        def step_k(c):
            await_(r1.at[c], a1r.at[c])
            for one in a0(c, False):
                one.start()

        def step_w(c):
            k, l, _ = todo[c]
            await_(ph.at[c], a0r.at[c])
            pltpu.make_async_copy(out[k].at[l, :, :, part(c)], ph.at[c], lp.at[c]).start()

        return dict(
            l=step_l, e=step_e, z0=step_z0, z1=step_z1, z2=step_z2, z3=step_z3, f=step_f,
            g=step_g, h=step_h, q=step_q, r=step_r, i=step_i, k=step_k, w=step_w,
        )

    for c in range(n):
        p0(c).start()
        for one in load_out(c):
            one.start()
    for c in range(n):
        for one in load_state(c):
            one.start()

    order = plan(n)
    for where in range(2):

        @pl.when(here == where)
        def _():
            take = steps(where == 0)
            for name, *args in order[where]:
                take[name](*args)
            for c in range(n):
                await_(r3.at[: (2, 10)[where]], gs.at[c])

    for c in range(n):
        await_(ph.at[c], lp.at[c])
        await_(ph.at[c], a0s.at[c])
        await_(ph.at[c], p0s.at[c])
        await_(r1.at[c], a1s.at[c])
        await_(r3.at[c], a3s.at[c])


def finish(*refs):
    r1, po, ph, mb, vb = refs[:5]
    new_w, new_m, new_v = (refs[i : i + 3] for i in (5, 8, 11))
    here, there, beside, state = refs[14:]
    me = lax.axis_index("dp")
    core, y, x = me % 2, me // 8 % 2, me // 16
    a = x * (1 - core) + y * core
    sa, sb = 2 - core, 1 + core
    copies = []
    for c, (k, l, o) in enumerate(chunks()):
        at = pl.ds(o, CUT)
        for j in range(2):
            copies.append(pltpu.make_async_copy(r1.at[c, j], new_w[k].at[l, a * sa + j * sb, :, core, at], here.at[c, j]))
            copies.append(pltpu.make_async_copy(po.at[c, j], new_w[k].at[l, (1 - a) * sa + j * sb, :, core, at], there.at[c, j]))
        copies.append(pltpu.make_async_copy(ph.at[c], new_w[k].at[l, :, :, 1 - core, at], beside.at[c]))
        copies.append(pltpu.make_async_copy(mb.at[c], new_m[k].at[l, at], state.at[c, 0]))
        copies.append(pltpu.make_async_copy(vb.at[c], new_v[k].at[l, at], state.at[c, 1]))
    for one in copies:
        one.start()
    for one in copies:
        one.wait()


def solution(mesh):
    shapes = ((40, 3072), (40, 3072), (96, 1280))
    n = len(chunks())
    any_ = pl.BlockSpec(memory_space=pl.ANY)

    def step(*arrays):
        g, w, m, v = (arrays[i : i + 3] for i in (0, 3, 6, 9))
        g = [tiled(one[0], (4, 4, 2), *s) for one, s in zip(g, shapes, strict=True)]
        w = [tiled(one, (4, 4, 2), *s) for one, s in zip(w, shapes, strict=True)]
        m = [tiled(one, (), *s) for one, s in zip(m, shapes, strict=True)]
        v = [tiled(one, (), *s) for one, s in zip(v, shapes, strict=True)]
        dma = lambda *shape: pltpu.SemaphoreType.DMA(shape)
        vmem = lambda *shape, dtype=BF16: pltpu.VMEM((*shape, 8, 128), dtype)
        shape = lambda *shape, dtype=BF16: jax.ShapeDtypeStruct((*shape, 8, 128), dtype)
        on_chip, off_chip = pl.BlockSpec(memory_space=pltpu.VMEM), pl.BlockSpec(memory_space=pltpu.HBM)
        keep = pltpu.with_memory_space_constraint
        *_, r1, po, ph, mb, vb = pl.pallas_call(
            kernel,
            out_shape=[pltpu.HBM((2, 4, 4, TILES, 8, 128), BF16)] * 6
            + [vmem(n, 2, 4, CUT), vmem(n, 2, 4, CUT), vmem(n, 4, 4, CUT), vmem(n, CUT, dtype=F32), vmem(n, CUT, dtype=F32)],
            in_specs=[any_] * 12,
            out_specs=[off_chip] * 6 + [on_chip] * 5,
            scratch_shapes=[
                vmem(3, 2, 4, CUT),
                vmem(n, 2, CUT),
                vmem(n, CUT),
                vmem(n, CUT),
                *(dma(n), dma(n), dma(n), dma(SLOTS), dma(n), dma(n)),
                *(dma(n), dma(n), dma(n), dma(n, 5), dma(n), dma(n), dma(n)),
                *(dma(n), dma(n, 3), dma(n), dma(n), dma(n), dma(n), dma(n)),
                pltpu.SemaphoreType.REGULAR((n,)),
            ],
            compiler_params=pltpu.CompilerParams(has_side_effects=True, vmem_limit_bytes=LIMIT),
        )(*g, *w, *m, *v)
        new = pl.pallas_call(
            finish,
            out_shape=[shape(2, 4, 4, 2, TILES)] * 3 + [shape(2, TILES, dtype=F32)] * 6,
            in_specs=[on_chip] * 5,
            out_specs=[any_] * 9,
            scratch_shapes=[dma(n, 2), dma(n, 2), dma(n), dma(n, 2)],
            compiler_params=pltpu.CompilerParams(vmem_limit_bytes=LIMIT),
        )(*(keep(one, pltpu.VMEM) for one in (r1, po, ph, mb, vb)))
        shape_of = lambda i: shapes[i % 3]
        return tuple(untiled(one, *shape_of(i)) for i, one in enumerate(new))

    all_of, cut = P(None, None, None), P(None, "dp", None)
    return jax.shard_map(
        step,
        mesh=mesh,
        in_specs=(P(("rep", "dp"), None, None, None),) * 3 + (all_of,) * 3 + (cut,) * 6,
        out_specs=(P("rep", None, None),) * 3 + (P("rep", "dp", None),) * 6,
        check_vma=False,
    )
```

time: 382 us -> 365 us (0.955)
  Pallas kernels: 380 us -> 363 us
    pallas_call x1, Pallas kernels: 355 us -> 345 us  [step(): pl.pallas_call(kernel, out_shape=[pltpu.HBM((2, 4, 4, TILES, 8, 128), BF1...]
    pallas_call x1, Pallas kernels: 25.9 us -> 17.9 us  [step(): pl.pallas_call(finish, out_shape=[shape(2, 4, 4, 2, TILES)] * 3 + [shape(...]
where the time goes in v3:
time: 365 us; the launch traced here: 363 us
  Pallas kernels  363 us (99%)
    pallas_call x1, Pallas kernels, step(): pl.pallas_call(kernel, out_shape=[pltpu.HBM((2, 4, 4, TILES, 8, 128), BF1...  345 us
    pallas_call x1, Pallas kernels, step(): pl.pallas_call(finish, out_shape=[shape(2, 4, 4, 2, TILES)] * 3 + [shape(...  17.9 us

profile of v3, /device:TPU:0, one launch (start us, length us, event | category | flops | bytes accessed | tf_op | source)
XLA Modules:
  0.0 363.5 jit_solution(7665918318964790732)
XLA Ops:
  0.6 344.8 %shard_map.187 = (bf16[2,4,4,120,8,128]{5,4,3,2,1,0:T(8,128)(2,1)}, bf16[2,4,4,120,8,128]{5,4,3,2,1,0:T(8,128)(2,1)}, bf16[2,4,4,120,8,128]{5,4,3,2,1,0:T(8,128)...) custom-call(bf16[2,4,4,2,120,8,128]{6,5,4,3,2,1,0:T(8,128)(2,1)} %bi, ...), custom_call_target="tpu_custom_call" | custom-call | tf_op jit(solution)/shard_map/pallas_call | solution.py:458
  345.4 17.9 %shard_map.188 = (bf16[2,4,4,2,120,8,128]{6,5,4,3,2,1,0:T(8,128)(2,1)}, bf16[2,4,4,2,120,8,128]{6,5,4,3,2,1,0:T(8,128)(2,1)}, bf16[2,4,4,2,120,8,128]{6,5,4,3,2,...) custom-call(bf16[18,2,4,40,8,128]{5,4,3,2,1,0:T(8,128)(2,1)S(1)} %ge, ...), custom_call_target="tpu_custom_call" | custom-call | tf_op jit(solution)/shard_map/pallas_call | solution.py:476

commit v4 on v3

--- a/solution.py
+++ b/solution.py
@@ -33,7 +33,7 @@
 
 def plan(n):
     tile = 2048e-3
-    hop, z_rate, x_rate, b_rate, pair_rate = 1.5, 46.6e3, 90e3, 46e3, 600e3
+    hop, z_rate, x_rate, b_rate, pair_rate = 2.0, 46.6e3, 80e3, 30e3, 540e3
     rank = dict(z1=0, z2=0, z3=0, z0=1, f=2, g=3, e=4, l=4, h=5, q=5.5, i=6, r=7, k=8, w=9)
     free, arrived, sent, now = {}, {}, {}, [0.0, 0.0]
     done = [{}, {}]

time: 365 us -> 353 us (0.967)
  Pallas kernels: 363 us -> 351 us
    pallas_call x1, Pallas kernels: 345 us -> 333 us  [step(): pl.pallas_call(kernel, out_shape=[pltpu.HBM((2, 4, 4, TILES, 8, 128), BF1...]
where the time goes in v4:
time: 353 us; the launch traced here: 351 us
  Pallas kernels  351 us (99%)
    pallas_call x1, Pallas kernels, step(): pl.pallas_call(kernel, out_shape=[pltpu.HBM((2, 4, 4, TILES, 8, 128), BF1...  333 us
    pallas_call x1, Pallas kernels, step(): pl.pallas_call(finish, out_shape=[shape(2, 4, 4, 2, TILES)] * 3 + [shape(...  17.9 us

profile of v4, /device:TPU:0, one launch (start us, length us, event | category | flops | bytes accessed | tf_op | source)
XLA Modules:
  0.0 351.4 jit_solution(9707150721329035484)
XLA Ops:
  0.6 332.7 %shard_map.187 = (bf16[2,4,4,120,8,128]{5,4,3,2,1,0:T(8,128)(2,1)}, bf16[2,4,4,120,8,128]{5,4,3,2,1,0:T(8,128)(2,1)}, bf16[2,4,4,120,8,128]{5,4,3,2,1,0:T(8,128)...) custom-call(bf16[2,4,4,2,120,8,128]{6,5,4,3,2,1,0:T(8,128)(2,1)} %bi, ...), custom_call_target="tpu_custom_call" | custom-call | tf_op jit(solution)/shard_map/pallas_call | solution.py:458
  333.3 17.9 %shard_map.188 = (bf16[2,4,4,2,120,8,128]{6,5,4,3,2,1,0:T(8,128)(2,1)}, bf16[2,4,4,2,120,8,128]{6,5,4,3,2,1,0:T(8,128)(2,1)}, bf16[2,4,4,2,120,8,128]{6,5,4,3,2,...) custom-call(bf16[18,2,4,40,8,128]{5,4,3,2,1,0:T(8,128)(2,1)S(1)} %ge, ...), custom_call_target="tpu_custom_call" | custom-call | tf_op jit(solution)/shard_map/pallas_call | solution.py:476
